TPU v7x, 32 devices: a whole 2x2x4 slice. The times are simulated.
32 devices in a mesh: samp: 4 (over z), seq: 8 (over y, x, core).
Axes of the slice: x: 2, y: 2, z: 4, core: 2. Of those that a mesh axis runs over, the one named last changes fastest.
Arguments:
- queries: bfloat16 [4, 4096, 3584], P('samp', 'seq'), may hold values from -200 to 200
- keys: bfloat16 [4, 4096, 512], P('samp', 'seq'), may hold values from -6 to 6
- values: bfloat16 [4, 4096, 512], P('samp', 'seq'), may hold values from -6 to 6
- reg_owner: int32 [4], P('samp'), may hold values from 0 to 7
- block_lists: int32 [4, 32, 8], P('samp', 'seq'), may hold values from 0 to 31, as said below
- list_counts: int32 [4, 32], P('samp', 'seq'), may hold values from 0 to 8, as said below
- image_blocks: int32 [4, 32], P('samp', 'seq'), may hold values from 0 to 1, as said below
Outputs:
- attended: bfloat16 [4, 4096, 3584], P('samp', 'seq')
Inputs may be any that keep to these rules, and one draw needn't show every extreme that they name: `block_lists`: block b lies on sequence index b // 4. Entry t of a list is used only where t < the block's count, unused entries are 0. The used entries of one block name blocks of distinct sequence indices other than its own. Over all blocks of one sequence index, at most one distinct block of each other sequence index is named. On the last sequence index of each sample, the lists together name a block of every other index. `list_counts`: 0 for image blocks; at most 8. `image_blocks`: the blocks of the last sequence index of each sample are text blocks.
All inputs are finite; a program needn't handle non-finite values.
Results may differ from a plain program's by a relative error of at most 0.0043.
Values may be sent and summed in bfloat16 or wider, within the bound.
No kernel may reach another device: no remote copies, remote signals or barrier semaphores. Data moves between devices by JAX's collectives and lax.ppermute only.
A program may use at most 128 MiB of HBM per device.

v0:
```python
import functools
import math

import jax
import jax.numpy as jnp
from jax import lax
from jax.experimental import pallas as pl
from jax.experimental.pallas import tpu as pltpu
from jax.sharding import PartitionSpec as P


QUERY_HEADS = 28
KEY_VALUE_HEADS = 4
HEAD_SIZE = 128
REG = 64
GROUP = QUERY_HEADS // KEY_VALUE_HEADS
ONES_ROWS = 16
CHUNKS = ((0, 1), (1, 1), (2, 2))
SELECT_VMEM = int(56 * 2**20)
ATTEND_VMEM = 67043328
SCORE_SCALE = math.log2(math.e) / math.sqrt(HEAD_SIZE)
LARGEST_POWER = 64.0
NT = (((1,), (1,)), ((), ()))
NN = (((1,), (0,)), ((), ()))


def select_kernel(chips, rows, me_ref, *refs):
    tables = refs[: chips - 1]
    own_k, own_v, mate_k, mate_v = refs[chips - 1 : chips + 3]
    sends = refs[chips + 3 : -3]
    held, read_sem, write_sem = refs[-3:]
    me = me_ref[0]
    blocks = own_k.shape[0] // rows
    reads = []
    for chip in range(chips - 1):
        table = tables[chip]
        for side, (keys, values) in enumerate(((own_k, own_v), (mate_k, mate_v))):
            base = (me ^ side) * blocks
            block = jnp.int32(0)
            for b in range(table.shape[0]):
                for t in range(table.shape[1]):
                    place = table[b, t] - base
                    block = jnp.where((place >= 0) & (place < blocks), place, block)
            start = pl.multiple_of(block * rows, rows)
            for i, source in enumerate((keys, values)):
                copy = pltpu.make_async_copy(
                    source.at[pl.ds(start, rows)],
                    held.at[chip, side, i],
                    read_sem.at[chip, side, i],
                )
                copy.start()
                reads.append(copy)
    writes = []
    for chip in range(chips - 1):
        for copy in reads[4 * chip : 4 * chip + 4]:
            copy.wait()
        for piece, (first, count) in enumerate(CHUNKS):
            cols = pl.ds(first * HEAD_SIZE, count * HEAD_SIZE)
            copy = pltpu.make_async_copy(
                held.at[chip, :, :, :, cols],
                sends[piece * (chips - 1) + chip],
                write_sem.at[piece, chip],
            )
            copy.start()
            writes.append(copy)
    for copy in writes:
        copy.wait()


def select_blocks(me, tables, own_k, own_v, mate_k, mate_v, rows):
    chips = len(tables) + 1
    smem = pl.BlockSpec(memory_space=pltpu.SMEM)
    anywhere = pl.BlockSpec(memory_space=pl.ANY)
    shapes = [
        jax.ShapeDtypeStruct((2, 2, rows, count * HEAD_SIZE), jnp.bfloat16)
        for _, count in CHUNKS
        for _ in range(chips - 1)
    ]
    return pl.pallas_call(
        functools.partial(select_kernel, chips, rows),
        in_specs=[smem] * chips + [anywhere] * 4,
        out_specs=[anywhere] * len(shapes),
        out_shape=shapes,
        scratch_shapes=[
            pltpu.VMEM((chips - 1, 2, 2, rows, own_k.shape[1]), jnp.bfloat16),
            pltpu.SemaphoreType.DMA((chips - 1, 2, 2)),
            pltpu.SemaphoreType.DMA((len(CHUNKS), chips - 1)),
        ],
        compiler_params=pltpu.CompilerParams(vmem_limit_bytes=SELECT_VMEM),
        name="select_blocks",
    )(me, *tables, own_k, own_v, mate_k, mate_v)


def attend_kernel(first, heads, received, rows, listed, image, me_ref, *refs):
    q_ref, own_k, own_v, mate_k, mate_v = refs[:5]
    arrived = refs[5 : 5 + received]
    reg_k, reg_v = refs[5 + received : 7 + received]
    refs = refs[7 + received :]
    if first > 0:
        refs = refs[1:]
    out_ref = refs[0]
    key_pool, value_pool, reg_value, p0, p1, q_buf, k_buf, v_buf = refs[1:9]
    mate_buf, far_buf, reg_buf, o_buf, sem, write_sem = refs[9:]
    weight_refs = (p0, p1)
    tokens = k_buf.shape[0]
    blocks = tokens // rows
    slots = listed.shape[1]
    reg = reg_buf.shape[1]
    fill = key_pool.shape[1] - 1
    width = GROUP * HEAD_SIZE
    me = me_ref[0]
    table = {}
    from_mate = jnp.int32(0)
    for b in range(blocks):
        for t in range(slots):
            entry = listed[b, t]
            away = (entry // blocks) ^ me
            table[b, t] = jnp.where(entry >= 0, blocks - 1 + away, fill)
            from_mate = jnp.where((entry >= 0) & (away == 1), entry % blocks, from_mate)
    start = pl.multiple_of(from_mate * rows, rows)
    cols = pl.ds(first * HEAD_SIZE, heads * HEAD_SIZE)
    moves = [
        (q_ref.at[:, pl.ds((first + h) * width, width)], q_buf.at[h]) for h in range(heads)
    ]
    moves += [
        (own_k.at[:, cols], k_buf),
        (own_v.at[:, cols], v_buf),
        (mate_k.at[pl.ds(start, rows), cols], mate_buf.at[0]),
        (mate_v.at[pl.ds(start, rows), cols], mate_buf.at[1]),
        (reg_k.at[:, cols], reg_buf.at[0]),
        (reg_v.at[:, cols], reg_buf.at[1]),
    ]
    moves += [(arrived[d], far_buf.at[d]) for d in range(received)]
    copies = [pltpu.make_async_copy(x, y, sem.at[i]) for i, (x, y) in enumerate(moves)]
    for copy in copies:
        copy.start()
    row_ids = lax.broadcasted_iota(jnp.int32, (ONES_ROWS, rows), 0)
    ones = jnp.where(row_ids == 0, 1.0, 0.0).astype(jnp.bfloat16)
    for h in range(heads):
        for slot in range(fill):
            value_pool[h, slot, HEAD_SIZE:] = ones
        value_pool[h, fill] = jnp.zeros(value_pool.shape[2:], jnp.bfloat16)
        reg_value[h, HEAD_SIZE:] = ones[:, :reg]
    for copy in copies[heads:] + copies[:1]:
        copy.wait()

    def build(h):
        own = slice(h * HEAD_SIZE, (h + 1) * HEAD_SIZE)

        def put(slot, keys, values):
            key_pool[h, slot] = keys
            value_pool[h, slot, :HEAD_SIZE] = values.T

        for b in range(blocks):
            at = slice(b * rows, (b + 1) * rows)
            put(b, k_buf[at, own], v_buf[at, own])
        put(blocks, mate_buf[0, :, own], mate_buf[1, :, own])
        for d in range(received):
            for side in range(2):
                put(
                    blocks + 1 + 2 * d + side,
                    far_buf[d, side, 0, :, own],
                    far_buf[d, side, 1, :, own],
                )
        for r in range(rows // reg):
            key_pool[h, fill, r * reg : (r + 1) * reg] = reg_buf[0, :, own]
        reg_value[h, :HEAD_SIZE] = reg_buf[1, :, own].T

    def reg_keys(h):
        return key_pool[h, fill, :reg]

    def write(h, b):
        return pltpu.make_async_copy(
            o_buf.at[h, b],
            out_ref.at[pl.ds(b * rows, rows), pl.ds((first + h) * width, width)],
            write_sem.at[h, b],
        )

    steps = [
        (h, b, 2 * j, min(2 * j + 2, GROUP))
        for h in range(heads)
        for b in range(blocks)
        for j in range((GROUP + 1) // 2)
    ]
    over = []

    def causal(b, wide):
        key_row = lax.broadcasted_iota(jnp.int32, (rows, wide), 0)
        query_row = lax.broadcasted_iota(jnp.int32, (rows, wide), 1) % rows
        return (key_row <= query_row) | (image[b] == 1)

    def weights(i):
        h, b, lo, hi = steps[i]
        wide = (hi - lo) * rows
        p_ref = weight_refs[i % 2]
        q = jnp.concatenate(
            [
                q_buf[h, b * rows : (b + 1) * rows, c * HEAD_SIZE : (c + 1) * HEAD_SIZE]
                for c in range(lo, hi)
            ],
            axis=0,
        )
        near_keys = jnp.concatenate([key_pool[h, b], reg_keys(h)], axis=0)
        far_keys = jnp.concatenate([key_pool[h, table[b, t]] for t in range(slots)], axis=0)
        near = lax.dot_general(near_keys, q, NT, preferred_element_type=jnp.float32)
        far = lax.dot_general(far_keys, q, NT, preferred_element_type=jnp.float32)
        own = jnp.where(causal(b, wide), near[:rows], -jnp.inf)
        base = jnp.maximum(
            jnp.max(own, axis=0, keepdims=True), jnp.max(near[rows:], axis=0, keepdims=True)
        )
        top = jnp.max(far.reshape(-1, 8, wide), axis=0) - base
        over.append(jnp.maximum(top[:, :rows], top[:, wide - rows :]))

        def weigh(s):
            return jnp.exp2((s - base) * SCORE_SCALE).astype(jnp.bfloat16)

        p_ref[:rows, :wide] = weigh(own)
        p_ref[rows:-reg, :wide] = weigh(far)
        p_ref[-reg:, :wide] = weigh(near[rows:])

    def gather_values(h, b, slot):
        return jnp.concatenate(
            [value_pool[h, b]]
            + [value_pool[h, slot(t)] for t in range(slots)]
            + [reg_value[h]],
            axis=1,
        )

    def normalized(values, p):
        o = lax.dot_general(values, p, NN, preferred_element_type=jnp.float32)
        return o[:HEAD_SIZE] * (1.0 / o[HEAD_SIZE : HEAD_SIZE + 1])

    def output(i):
        h, b, lo, hi = steps[i]
        wide = (hi - lo) * rows
        values = gather_values(h, b, lambda t: table[b, t])
        o = normalized(values, weight_refs[i % 2][:, :wide])
        for c in range(lo, hi):
            o_buf[h, b, :, c * HEAD_SIZE : (c + 1) * HEAD_SIZE] = (
                o[:, (c - lo) * rows : (c - lo + 1) * rows].T.astype(jnp.bfloat16)
            )
        if hi == GROUP:
            write(h, b).start()

    build(0)
    count = len(steps)
    for i in range(count + 1):
        if i < count:
            if i > 0 and steps[i][0] != steps[i - 1][0]:
                copies[steps[i][0]].wait()
                build(steps[i][0])
            weights(i)
        if i >= 1:
            output(i - 1)
    for h in range(heads):
        for b in range(blocks):
            write(h, b).wait()

    worst = over[0]
    for other in over[1:]:
        worst = jnp.maximum(worst, other)

    @pl.when(jnp.max(worst) * SCORE_SCALE > LARGEST_POWER)
    def _():
        for h in range(heads):

            def exact(n, carry):
                b = n // GROUP
                at = pl.ds(pl.multiple_of(b * rows, rows), rows)
                lanes = pl.ds(pl.multiple_of((n % GROUP) * HEAD_SIZE, HEAD_SIZE), HEAD_SIZE)

                def slot(t):
                    entry = listed[b, t]
                    return jnp.where(entry >= 0, blocks - 1 + ((entry // blocks) ^ me), fill)

                keys = jnp.concatenate(
                    [key_pool[h, b]]
                    + [key_pool[h, slot(t)] for t in range(slots)]
                    + [reg_keys(h)],
                    axis=0,
                )
                s = lax.dot_general(
                    keys, q_buf[h, at, lanes], NT, preferred_element_type=jnp.float32
                )
                s = jnp.concatenate(
                    [jnp.where(causal(b, rows), s[:rows], -jnp.inf), s[rows:]], axis=0
                )
                p = jnp.exp2((s - jnp.max(s, axis=0, keepdims=True)) * SCORE_SCALE)
                o = normalized(gather_values(h, b, slot), p.astype(jnp.bfloat16))
                o_buf[h, b, :, lanes] = o.T.astype(jnp.bfloat16)
                return carry

            lax.fori_loop(0, blocks * GROUP, exact, 0)
            for b in range(blocks):
                write(h, b).start()
                write(h, b).wait()


def attend(listed, image, me, q, own_k, own_v, mate_k, mate_v, arrived, regs, out, chunk):
    first, heads = chunk
    tokens = q.shape[0]
    blocks, slots = listed.shape
    rows = tokens // blocks
    reg = regs[0].shape[0]
    pool = blocks + 2 + 2 * len(arrived)
    keys = rows * (1 + slots) + reg
    smem = pl.BlockSpec(memory_space=pltpu.SMEM)
    anywhere = pl.BlockSpec(memory_space=pl.ANY)
    operands = [listed, image, me, q, own_k, own_v, mate_k, mate_v, *arrived, *regs]
    aliases = {}
    if first > 0:
        aliases = {len(operands): 0}
        operands.append(out)
    bf16 = jnp.bfloat16
    cols = heads * HEAD_SIZE
    return pl.pallas_call(
        functools.partial(attend_kernel, first, heads, len(arrived), rows),
        in_specs=[smem] * 3 + [anywhere] * (len(operands) - 3),
        out_specs=anywhere,
        out_shape=jax.ShapeDtypeStruct(q.shape, bf16),
        scratch_shapes=[
            pltpu.VMEM((heads, pool, rows, HEAD_SIZE), bf16),
            pltpu.VMEM((heads, pool, HEAD_SIZE + ONES_ROWS, rows), bf16),
            pltpu.VMEM((heads, HEAD_SIZE + ONES_ROWS, reg), bf16),
            pltpu.VMEM((keys, 2 * rows), bf16),
            pltpu.VMEM((keys, 2 * rows), bf16),
            pltpu.VMEM((heads, tokens, GROUP * HEAD_SIZE), bf16),
            pltpu.VMEM((tokens, cols), bf16),
            pltpu.VMEM((tokens, cols), bf16),
            pltpu.VMEM((2, rows, cols), bf16),
            pltpu.VMEM((len(arrived), 2, 2, rows, cols), bf16),
            pltpu.VMEM((2, reg, cols), bf16),
            pltpu.VMEM((heads, blocks, rows, GROUP * HEAD_SIZE), bf16),
            pltpu.SemaphoreType.DMA((heads + 6 + len(arrived),)),
            pltpu.SemaphoreType.DMA((heads, blocks)),
        ],
        input_output_aliases=aliases,
        compiler_params=pltpu.CompilerParams(vmem_limit_bytes=ATTEND_VMEM),
        cost_estimate=pl.CostEstimate(
            flops=4 * heads * GROUP * tokens * keys * HEAD_SIZE,
            bytes_accessed=4 * heads * GROUP * tokens * HEAD_SIZE,
            transcendentals=heads * GROUP * tokens * keys,
        ),
    )(*operands)


def layer(queries, keys, values, reg_owner, block_lists, list_counts, image_blocks):
    q = queries[0]
    own_k = keys[0]
    own_v = values[0]
    lists = block_lists[0]
    counts = list_counts[0]
    devices = lax.axis_size("seq")
    chips = devices // 2
    me = lax.axis_index("seq")
    blocks = lists.shape[0]
    slots = min(lists.shape[1], devices - 1)
    rows = own_k.shape[0] // blocks

    def swap(x, offset):
        return lax.ppermute(x, "seq", [(i, i ^ offset) for i in range(devices)])

    live = jnp.arange(slots, dtype=jnp.int32)[None, :] < counts[:, None]
    listed = jnp.where(live, lists[:, :slots], -1)
    tables = [swap(listed, 2 * d) for d in range(1, chips)]
    mate_k = swap(own_k, 1)
    mate_v = swap(own_v, 1)
    root = reg_owner[0]
    low = me % 2 == 0
    at_mate = (root ^ me) % 2 == 1
    half = jnp.where(
        low,
        jnp.where(at_mate, mate_k[:REG], own_k[:REG]),
        jnp.where(at_mate, mate_v[:REG], own_v[:REG]),
    )
    sends = select_blocks(
        me.reshape(1), tables, own_k, own_v, mate_k, mate_v, rows
    )
    arrived = [
        [swap(sends[piece * (chips - 1) + d - 1], 2 * d) for d in range(1, chips)]
        for piece in range(len(CHUNKS))
    ]
    found = half
    for d in range(1, chips):
        found = jnp.where((root ^ me) // 2 == d, swap(half, 2 * d), found)
    other = swap(found, 1)
    regs = (jnp.where(low, found, other), jnp.where(low, other, found))

    out = None
    for piece, chunk in enumerate(CHUNKS):
        out = attend(
            listed,
            image_blocks[0],
            me.reshape(1),
            q,
            own_k,
            own_v,
            mate_k,
            mate_v,
            arrived[piece],
            regs,
            out,
            chunk,
        )
    return out[None]


def solution(mesh):
    placed = (
        P("samp", "seq", None),
        P("samp", "seq", None),
        P("samp", "seq", None),
        P("samp"),
        P("samp", "seq", None),
        P("samp", "seq"),
        P("samp", "seq"),
    )
    return jax.shard_map(
        layer, mesh=mesh, in_specs=placed, out_specs=P("samp", "seq", None), check_vma=False
    )
```

profile of v0, /device:TPU:0, one launch (start us, length us, event | category | flops | bytes accessed | tf_op | source)
XLA Modules:
  0.0 66.6 jit_solution(2729926414396450405)
XLA Ops:
  0.0 0.5 collective-permute-start
  0.5 0.0 collective-permute-start.1
  1.2 1.1 %collective-permute-done.refs_5_.refs_3_ = bf16[512,512]{1,0:T(8,128)(2,1)S(1)} collective-permute-done((bf16[512,512]{1,0:T(8,128)(2,1)}, bf16[512,512]{1,0:T(8,128)(2,1)S(1)}, u32[]{:S(2)}, u32[]{:S(2)}) %collective-permute-start) | collective-permute-done | bytes 524320 | tf_op jit(solution)/shard_map/ppermute | solution.py:361
  2.2 0.7 %collective-permute-done.1.refs_6_.refs_4_ = bf16[512,512]{1,0:T(8,128)(2,1)S(1)} collective-permute-done((bf16[512,512]{1,0:T(8,128)(2,1)}, bf16[512,512]{1,0:T(8,128)(2,1)S(1)}, u32[]{:S(2)}, u32[]{:S(2)}) %collective-permute-start.1) | collective-permute-done | bytes 524320 | tf_op jit(solution)/shard_map/ppermute | solution.py:361
  3.0 1.0 %fusion = bf16[64,512]{1,0:T(8,128)(2,1)S(1)} fusion(bf16[512,512]{1,0:T(8,128)(2,1)S(1)} %collective-permute-done.1.refs_6_.refs_4_, bf16[512,512]{1,0:T(8,128)(2,1)S(1)} %collective-permute-done.refs_5_.refs_3_, bf16[1,512,512]{2,1,0:T(8,128)(2,1)} %param.9, bf16[1,512,512]{2,1,0:T(8,128)(2,1)} %param.8, pred[]{:T(512)S(6)} %eq.20, pred[]{:T(512)S(6)} %eq.18), kind=kLoop, calls=%fused_computation.1 | loop fusion | flops 98304 | bytes 327682 | tf_op jit(solution)/shard_map/jit(_where)/select_n | solution.py:371
  4.0 2.9 %collective-permute-start.10 = (bf16[64,512]{1,0:T(8,128)(2,1)S(1)}, bf16[64,512]{1,0:T(8,128)(2,1)S(1)}, u32[]{:S(2)}, u32[]{:S(2)}) collective-permute-start(bf16[64,512]{1,0:T(8,128)(2,1)S(1)} %fusion), channel_id=1, source_target_pairs={{0,2},{1,3},{2,0},{3,1},{4,6},{5,7},{6,4},{7,5},{8,10},{9,11},{10,... | collective-permute-start | bytes 196616 | tf_op jit(solution)/shard_map/ppermute | solution.py:361
  6.9 1.5 %collective-permute-start.9 = (bf16[64,512]{1,0:T(8,128)(2,1)S(1)}, bf16[64,512]{1,0:T(8,128)(2,1)S(1)}, u32[]{:S(2)}, u32[]{:S(2)}) collective-permute-start(bf16[64,512]{1,0:T(8,128)(2,1)S(1)} %fusion), channel_id=1, source_target_pairs={{0,4},{1,5},{2,6},{3,7},{4,0},{5,1},{6,2},{7,3},{8,12},{9,13},{10,... | collective-permute-start | bytes 196616 | tf_op jit(solution)/shard_map/ppermute | solution.py:361
  8.4 0.0 collective-permute-start.8
  8.5 0.9 %collective-permute-done.10 = bf16[64,512]{1,0:T(8,128)(2,1)S(1)} collective-permute-done((bf16[64,512]{1,0:T(8,128)(2,1)S(1)}, bf16[64,512]{1,0:T(8,128)(2,1)S(1)}, u32[]{:S(2)}, u32[]{:S(2)}) %collective-permute-start.10) | collective-permute-done | bytes 65568 | tf_op jit(solution)/shard_map/ppermute | solution.py:361
  9.3 1.9 %collective-permute-done.9 = bf16[64,512]{1,0:T(8,128)(2,1)S(1)} collective-permute-done((bf16[64,512]{1,0:T(8,128)(2,1)S(1)}, bf16[64,512]{1,0:T(8,128)(2,1)S(1)}, u32[]{:S(2)}, u32[]{:S(2)}) %collective-permute-start.9) | collective-permute-done | bytes 65568 | tf_op jit(solution)/shard_map/ppermute | solution.py:361
  11.2 2.4 %collective-permute-done.8 = bf16[64,512]{1,0:T(8,128)(2,1)S(1)} collective-permute-done((bf16[64,512]{1,0:T(8,128)(2,1)S(1)}, bf16[64,512]{1,0:T(8,128)(2,1)S(1)}, u32[]{:S(2)}, u32[]{:S(2)}) %collective-permute-start.8) | collective-permute-done | bytes 65568 | tf_op jit(solution)/shard_map/ppermute | solution.py:361
  13.6 0.1 collective-permute-start.11
  13.7 0.8 %slice_select_fusion.2.listed = s32[4,7]{1,0:T(4,128)S(1)} fusion(s32[4,8]{1,0:T(4,128)} %bitcast.30, s32[4]{0:T(128)} %bitcast.31), kind=kLoop, calls=%fused_computation.6 | loop fusion | flops 56 | bytes 240 | tf_op jit(solution)/shard_map/jit(_where)/select_n | solution.py:364
  14.5 0.4 collective-permute-start.4
  14.9 1.6 %collective-permute-start.3 = (s32[4,7]{1,0:T(4,128)S(1)}, s32[4,7]{1,0:T(4,128)S(1)}, u32[]{:S(2)}, u32[]{:S(2)}) collective-permute-start(s32[4,7]{1,0:T(4,128)S(1)} %slice_select_fusion.2.listed), channel_id=1, source_target_pairs={{0,4},{1,5},{2,6},{3,7},{4,0},{5,1},{6,2},{7,3},{8,12},{9,13},{10,... | collective-permute-start | bytes 344 | tf_op jit(solution)/shard_map/ppermute | solution.py:361
  16.5 1.5 %collective-permute-start.2 = (s32[4,7]{1,0:T(4,128)S(1)}, s32[4,7]{1,0:T(4,128)S(1)}, u32[]{:S(2)}, u32[]{:S(2)}) collective-permute-start(s32[4,7]{1,0:T(4,128)S(1)} %slice_select_fusion.2.listed), channel_id=1, source_target_pairs={{0,2},{1,3},{2,0},{3,1},{4,6},{5,7},{6,4},{7,5},{8,10},{9,11},{10,... | collective-permute-start | bytes 344 | tf_op jit(solution)/shard_map/ppermute | solution.py:361
  17.9 1.0 %collective-permute-done.4.refs_2_ = s32[4,7]{1,0:T(4,128)S(1)} collective-permute-done((s32[4,7]{1,0:T(4,128)S(1)}, s32[4,7]{1,0:T(4,128)S(1)}, u32[]{:S(2)}, u32[]{:S(2)}) %collective-permute-start.4) | collective-permute-done | bytes 144 | tf_op jit(solution)/shard_map/ppermute | solution.py:361
  18.9 0.0 collective-permute-done.3.refs_1_
  18.9 1.1 %collective-permute-done.2.refs_0_ = s32[4,7]{1,0:T(4,128)S(1)} collective-permute-done((s32[4,7]{1,0:T(4,128)S(1)}, s32[4,7]{1,0:T(4,128)S(1)}, u32[]{:S(2)}, u32[]{:S(2)}) %collective-permute-start.2) | collective-permute-done | bytes 144 | tf_op jit(solution)/shard_map/ppermute | solution.py:361
  20.0 0.0 copy-done
  20.0 0.0 copy-done.1
  20.0 0.0 copy-done.3
  20.1 0.6 copy-done.5
  20.6 3.3 %select_blocks.1 = (bf16[2,2,128,128]{3,2,1,0:T(8,128)(2,1)}, bf16[2,2,128,128]{3,2,1,0:T(8,128)(2,1)}, bf16[2,2,128,128]{3,2,1,0:T(8,128)(2,1)}, bf16[2,2,128,1...) custom-call(s32[1]{0:T(128)} %bitcast.3.me_ref, ...), custom_call_target="tpu_custom_call" | custom-call | tf_op jit(solution)/shard_map/select_blocks/pallas_call | solution.py:79
  23.9 1.6 %collective-permute-start.12 = (bf16[2,2,128,128]{3,2,1,0:T(8,128)(2,1)}, bf16[2,2,128,128]{3,2,1,0:T(8,128)(2,1)}, u32[]{:S(2)}, u32[]{:S(2)}) collective-permute-start(bf16[2,2,128,128]{3,2,1,0:T(8,128)(2,1)} %get-tuple-element.17), channel_id=1, source_target_pairs={{0,2},{1,3},{2,0},{3,1},{4,6},{5,7},{6,4},{7,5},{8,10},{9,11},{10,... | collective-permute-start | bytes 393224 | tf_op jit(solution)/shard_map/ppermute | solution.py:361
  25.5 0.5 collective-permute-start.13
  26.0 0.5 collective-permute-start.15
  26.4 1.6 %collective-permute-start.16 = (bf16[2,2,128,128]{3,2,1,0:T(8,128)(2,1)}, bf16[2,2,128,128]{3,2,1,0:T(8,128)(2,1)}, u32[]{:S(2)}, u32[]{:S(2)}) collective-permute-start(bf16[2,2,128,128]{3,2,1,0:T(8,128)(2,1)} %get-tuple-element.21), channel_id=1, source_target_pairs={{0,4},{1,5},{2,6},{3,7},{4,0},{5,1},{6,2},{7,3},{8,12},{9,13},{10,... | collective-permute-start | bytes 393224 | tf_op jit(solution)/shard_map/ppermute | solution.py:361
  28.0 0.0 collective-permute-done.11
  28.0 1.4 %collective-permute-start.17 = (bf16[2,2,128,128]{3,2,1,0:T(8,128)(2,1)}, bf16[2,2,128,128]{3,2,1,0:T(8,128)(2,1)}, u32[]{:S(2)}, u32[]{:S(2)}) collective-permute-start(bf16[2,2,128,128]{3,2,1,0:T(8,128)(2,1)} %get-tuple-element.22), channel_id=1, source_target_pairs={{0,6},{1,7},{2,4},{3,5},{4,2},{5,3},{6,0},{7,1},{8,14},{9,15},{10,... | collective-permute-start | bytes 393224 | tf_op jit(solution)/shard_map/ppermute | solution.py:361
  29.5 0.7 broadcast_select_fusion
  30.1 0.0 copy-done.2
  30.1 0.5 collective-permute-done.12.refs_5_
  30.7 1.4 %collective-permute-start.14 = (bf16[2,2,128,128]{3,2,1,0:T(8,128)(2,1)}, bf16[2,2,128,128]{3,2,1,0:T(8,128)(2,1)}, u32[]{:S(2)}, u32[]{:S(2)}) collective-permute-start(bf16[2,2,128,128]{3,2,1,0:T(8,128)(2,1)} %get-tuple-element.19), channel_id=1, source_target_pairs={{0,6},{1,7},{2,4},{3,5},{4,2},{5,3},{6,0},{7,1},{8,14},{9,15},{10,... | collective-permute-start | bytes 393224 | tf_op jit(solution)/shard_map/ppermute | solution.py:361
  32.1 1.4 %collective-permute-done.15.refs_5_ = bf16[2,2,128,128]{3,2,1,0:T(8,128)(2,1)} collective-permute-done((bf16[2,2,128,128]{3,2,1,0:T(8,128)(2,1)}, bf16[2,2,128,128]{3,2,1,0:T(8,128)(2,1)}, u32[]{:S(2)}, u32[]{:S(2)}) %collective-permute-start.15) | collective-permute-done | bytes 131104 | tf_op jit(solution)/shard_map/ppermute | solution.py:361
  33.5 1.5 %collective-permute-start.5 = (bf16[2,2,128,256]{3,2,1,0:T(8,128)(2,1)}, bf16[2,2,128,256]{3,2,1,0:T(8,128)(2,1)}, u32[]{:S(2)}, u32[]{:S(2)}) collective-permute-start(bf16[2,2,128,256]{3,2,1,0:T(8,128)(2,1)} %get-tuple-element.14), channel_id=1, source_target_pairs={{0,2},{1,3},{2,0},{3,1},{4,6},{5,7},{6,4},{7,5},{8,10},{9,11},{10,... | collective-permute-start | bytes 786440 | tf_op jit(solution)/shard_map/ppermute | solution.py:361
  35.0 4.0 %collective-permute-done.16.refs_6_ = bf16[2,2,128,128]{3,2,1,0:T(8,128)(2,1)} collective-permute-done((bf16[2,2,128,128]{3,2,1,0:T(8,128)(2,1)}, bf16[2,2,128,128]{3,2,1,0:T(8,128)(2,1)}, u32[]{:S(2)}, u32[]{:S(2)}) %collective-permute-start.16) | collective-permute-done | bytes 131104 | tf_op jit(solution)/shard_map/ppermute | solution.py:361
  38.9 0.0 collective-permute-start.6
  38.9 0.0 collective-permute-done.17.refs_7_
  38.9 0.2 collective-permute-start.7
  39.1 7.4 %shard_map.73.refs_10_ = bf16[512,3584]{1,0:T(8,128)(2,1)} custom-call(s32[4,7]{1,0:T(4,128)} %copy-done.2, s32[4]{0:T(128)} %bitcast.27, s32[1]{0:T(128)} %bitcast.3.me_ref, bf16[512,3584]{1,0:T(8,128)(2,1)} %bitcast.14, bf16[512,512]{1,0:T(8,128)(2,1)} %bitcast.19, bf16[512,512]{1,0:T(8,128)(2,1)} %bitcast.24, bf16[512,512]{1,0:T(8,128)(2,1)} %copy-done, ...), custom_call_target="tpu_custom_call" | custom-call | flops 1996488704 | bytes 1835008 | tf_op jit(solution)/shard_map/pallas_call | solution.py:316
  46.5 0.0 collective-permute-done.13.refs_6_
  46.5 0.0 collective-permute-done.14.refs_7_
  46.5 7.6 %shard_map.74.refs_10_ = bf16[512,3584]{1,0:T(8,128)(2,1)} custom-call(s32[4,7]{1,0:T(4,128)} %copy-done.2, s32[4]{0:T(128)} %bitcast.28, s32[1]{0:T(128)} %bitcast.3.me_ref, bf16[512,3584]{1,0:T(8,128)(2,1)} %bitcast.15, bf16[512,512]{1,0:T(8,128)(2,1)} %bitcast.20, bf16[512,512]{1,0:T(8,128)(2,1)} %bitcast.25, ...), custom_call_target="tpu_custom_call", output_to_operand_aliasing={{}: (13, {})} | custom-call | flops 1996488704 | bytes 1835008 | tf_op jit(solution)/shard_map/pallas_call | solution.py:316
  54.1 0.0 collective-permute-done.5.refs_5_
  54.1 0.0 collective-permute-done.6.refs_6_
  54.2 0.0 collective-permute-done.7.refs_7_
  54.2 12.3 %shard_map.75 = bf16[512,3584]{1,0:T(8,128)(2,1)} custom-call(s32[4,7]{1,0:T(4,128)} %copy-done.2, s32[4]{0:T(128)} %bitcast.29, s32[1]{0:T(128)} %bitcast.3.me_ref, bf16[512,3584]{1,0:T(8,128)(2,1)} %bitcast.16, bf16[512,512]{1,0:T(8,128)(2,1)} %bitcast.21, bf16[512,512]{1,0:T(8,128)(2,1)} %bitcast.26, ...), custom_call_target="tpu_custom_call", output_to_operand_aliasing={{}: (13, {})} | custom-call | flops 3992977408 | bytes 3670016 | tf_op jit(solution)/shard_map/pallas_call | solution.py:316
  (8 shorter events, 0.0 us)
Async XLA Ops:
  0.0 2.2 %collective-permute-start = (bf16[512,512]{1,0:T(8,128)(2,1)}, bf16[512,512]{1,0:T(8,128)(2,1)S(1)}, u32[]{:S(2)}, u32[]{:S(2)}) collective-permute-start(bf16[512,512]{1,0:T(8,128)(2,1)} %bitcast.17), channel_id=1, source_target_pairs={{0,1},{1,0},{2,3},{3,2},{4,5},{5,4},{6,7},{7,6},{8,9},{9,8},{10,11... | collective-permute-start | bytes 1572872 | tf_op jit(solution)/shard_map/ppermute | solution.py:361
  0.5 2.5 %collective-permute-start.1 = (bf16[512,512]{1,0:T(8,128)(2,1)}, bf16[512,512]{1,0:T(8,128)(2,1)S(1)}, u32[]{:S(2)}, u32[]{:S(2)}) collective-permute-start(bf16[512,512]{1,0:T(8,128)(2,1)} %bitcast.22), channel_id=1, source_target_pairs={{0,1},{1,0},{2,3},{3,2},{4,5},{5,4},{6,7},{7,6},{8,9},{9,8},{10,11... | collective-permute-start | bytes 1572872 | tf_op jit(solution)/shard_map/ppermute | solution.py:361
  2.2 17.8 %copy-start = (bf16[512,512]{1,0:T(8,128)(2,1)}, bf16[512,512]{1,0:T(8,128)(2,1)S(1)}, u32[]{:S(2)}) copy-start(bf16[512,512]{1,0:T(8,128)(2,1)S(1)} %collective-permute-done.refs_5_.refs_3_) | copy-start | bytes 1572868
  3.0 17.1 %copy-start.1 = (bf16[512,512]{1,0:T(8,128)(2,1)}, bf16[512,512]{1,0:T(8,128)(2,1)S(1)}, u32[]{:S(2)}) copy-start(bf16[512,512]{1,0:T(8,128)(2,1)S(1)} %collective-permute-done.1.refs_6_.refs_4_) | copy-start | bytes 1572868
  4.0 5.3 %collective-permute-start.10 = (bf16[64,512]{1,0:T(8,128)(2,1)S(1)}, bf16[64,512]{1,0:T(8,128)(2,1)S(1)}, u32[]{:S(2)}, u32[]{:S(2)}) collective-permute-start(bf16[64,512]{1,0:T(8,128)(2,1)S(1)} %fusion), channel_id=1, source_target_pairs={{0,2},{1,3},{2,0},{3,1},{4,6},{5,7},{6,4},{7,5},{8,10},{9,11},{10,... | collective-permute-start | bytes 196616 | tf_op jit(solution)/shard_map/ppermute | solution.py:361
  6.9 4.3 %collective-permute-start.9 = (bf16[64,512]{1,0:T(8,128)(2,1)S(1)}, bf16[64,512]{1,0:T(8,128)(2,1)S(1)}, u32[]{:S(2)}, u32[]{:S(2)}) collective-permute-start(bf16[64,512]{1,0:T(8,128)(2,1)S(1)} %fusion), channel_id=1, source_target_pairs={{0,4},{1,5},{2,6},{3,7},{4,0},{5,1},{6,2},{7,3},{8,12},{9,13},{10,... | collective-permute-start | bytes 196616 | tf_op jit(solution)/shard_map/ppermute | solution.py:361
  8.4 5.2 %collective-permute-start.8 = (bf16[64,512]{1,0:T(8,128)(2,1)S(1)}, bf16[64,512]{1,0:T(8,128)(2,1)S(1)}, u32[]{:S(2)}, u32[]{:S(2)}) collective-permute-start(bf16[64,512]{1,0:T(8,128)(2,1)S(1)} %fusion), channel_id=1, source_target_pairs={{0,6},{1,7},{2,4},{3,5},{4,2},{5,3},{6,0},{7,1},{8,14},{9,15},{10,... | collective-permute-start | bytes 196616 | tf_op jit(solution)/shard_map/ppermute | solution.py:361
  13.6 14.4 %collective-permute-start.11 = (bf16[64,512]{1,0:T(8,128)(2,1)S(1)}, bf16[64,512]{1,0:T(8,128)(2,1)S(1)}, u32[]{:S(2)}, u32[]{:S(2)}) collective-permute-start(bf16[64,512]{1,0:T(8,128)(2,1)S(1)} %select_select_fusion), channel_id=1, source_target_pairs={{0,1},{1,0},{2,3},{3,2},{4,5},{5,4},{6,7},{7,6},{8,9},{9,8},{10,11... | collective-permute-start | bytes 196616 | tf_op jit(solution)/shard_map/ppermute | solution.py:361
  14.5 15.7 %copy-start.2 = (s32[4,7]{1,0:T(4,128)}, s32[4,7]{1,0:T(4,128)S(1)}, u32[]{:S(2)}) copy-start(s32[4,7]{1,0:T(4,128)S(1)} %slice_select_fusion.2.listed) | copy-start | bytes 340
  14.5 4.5 %collective-permute-start.4 = (s32[4,7]{1,0:T(4,128)S(1)}, s32[4,7]{1,0:T(4,128)S(1)}, u32[]{:S(2)}, u32[]{:S(2)}) collective-permute-start(s32[4,7]{1,0:T(4,128)S(1)} %slice_select_fusion.2.listed), channel_id=1, source_target_pairs={{0,6},{1,7},{2,4},{3,5},{4,2},{5,3},{6,0},{7,1},{8,14},{9,15},{10,... | collective-permute-start | bytes 344 | tf_op jit(solution)/shard_map/ppermute | solution.py:361
  14.9 4.1 %collective-permute-start.3 = (s32[4,7]{1,0:T(4,128)S(1)}, s32[4,7]{1,0:T(4,128)S(1)}, u32[]{:S(2)}, u32[]{:S(2)}) collective-permute-start(s32[4,7]{1,0:T(4,128)S(1)} %slice_select_fusion.2.listed), channel_id=1, source_target_pairs={{0,4},{1,5},{2,6},{3,7},{4,0},{5,1},{6,2},{7,3},{8,12},{9,13},{10,... | collective-permute-start | bytes 344 | tf_op jit(solution)/shard_map/ppermute | solution.py:361
  16.5 3.6 %collective-permute-start.2 = (s32[4,7]{1,0:T(4,128)S(1)}, s32[4,7]{1,0:T(4,128)S(1)}, u32[]{:S(2)}, u32[]{:S(2)}) collective-permute-start(s32[4,7]{1,0:T(4,128)S(1)} %slice_select_fusion.2.listed), channel_id=1, source_target_pairs={{0,2},{1,3},{2,0},{3,1},{4,6},{5,7},{6,4},{7,5},{8,10},{9,11},{10,... | collective-permute-start | bytes 344 | tf_op jit(solution)/shard_map/ppermute | solution.py:361
  18.9 1.1 %copy-start.3 = (s32[4,7]{1,0:T(4,128)}, s32[4,7]{1,0:T(4,128)S(1)}, u32[]{:S(2)}) copy-start(s32[4,7]{1,0:T(4,128)S(1)} %collective-permute-done.4.refs_2_) | copy-start | bytes 340
  18.9 1.1 %copy-start.4 = (s32[4,7]{1,0:T(4,128)}, s32[4,7]{1,0:T(4,128)S(1)}, u32[]{:S(2)}) copy-start(s32[4,7]{1,0:T(4,128)S(1)} %collective-permute-done.3.refs_1_) | copy-start | bytes 340
  20.0 0.6 copy-start.5
  23.9 6.8 %collective-permute-start.12 = (bf16[2,2,128,128]{3,2,1,0:T(8,128)(2,1)}, bf16[2,2,128,128]{3,2,1,0:T(8,128)(2,1)}, u32[]{:S(2)}, u32[]{:S(2)}) collective-permute-start(bf16[2,2,128,128]{3,2,1,0:T(8,128)(2,1)} %get-tuple-element.17), channel_id=1, source_target_pairs={{0,2},{1,3},{2,0},{3,1},{4,6},{5,7},{6,4},{7,5},{8,10},{9,11},{10,... | collective-permute-start | bytes 393224 | tf_op jit(solution)/shard_map/ppermute | solution.py:361
  25.5 21.0 %collective-permute-start.13 = (bf16[2,2,128,128]{3,2,1,0:T(8,128)(2,1)}, bf16[2,2,128,128]{3,2,1,0:T(8,128)(2,1)}, u32[]{:S(2)}, u32[]{:S(2)}) collective-permute-start(bf16[2,2,128,128]{3,2,1,0:T(8,128)(2,1)} %get-tuple-element.18), channel_id=1, source_target_pairs={{0,4},{1,5},{2,6},{3,7},{4,0},{5,1},{6,2},{7,3},{8,12},{9,13},{10,... | collective-permute-start | bytes 393224 | tf_op jit(solution)/shard_map/ppermute | solution.py:361
  26.0 7.5 %collective-permute-start.15 = (bf16[2,2,128,128]{3,2,1,0:T(8,128)(2,1)}, bf16[2,2,128,128]{3,2,1,0:T(8,128)(2,1)}, u32[]{:S(2)}, u32[]{:S(2)}) collective-permute-start(bf16[2,2,128,128]{3,2,1,0:T(8,128)(2,1)} %get-tuple-element.20), channel_id=1, source_target_pairs={{0,2},{1,3},{2,0},{3,1},{4,6},{5,7},{6,4},{7,5},{8,10},{9,11},{10,... | collective-permute-start | bytes 393224 | tf_op jit(solution)/shard_map/ppermute | solution.py:361
  26.4 12.5 %collective-permute-start.16 = (bf16[2,2,128,128]{3,2,1,0:T(8,128)(2,1)}, bf16[2,2,128,128]{3,2,1,0:T(8,128)(2,1)}, u32[]{:S(2)}, u32[]{:S(2)}) collective-permute-start(bf16[2,2,128,128]{3,2,1,0:T(8,128)(2,1)} %get-tuple-element.21), channel_id=1, source_target_pairs={{0,4},{1,5},{2,6},{3,7},{4,0},{5,1},{6,2},{7,3},{8,12},{9,13},{10,... | collective-permute-start | bytes 393224 | tf_op jit(solution)/shard_map/ppermute | solution.py:361
  28.0 10.9 %collective-permute-start.17 = (bf16[2,2,128,128]{3,2,1,0:T(8,128)(2,1)}, bf16[2,2,128,128]{3,2,1,0:T(8,128)(2,1)}, u32[]{:S(2)}, u32[]{:S(2)}) collective-permute-start(bf16[2,2,128,128]{3,2,1,0:T(8,128)(2,1)} %get-tuple-element.22), channel_id=1, source_target_pairs={{0,6},{1,7},{2,4},{3,5},{4,2},{5,3},{6,0},{7,1},{8,14},{9,15},{10,... | collective-permute-start | bytes 393224 | tf_op jit(solution)/shard_map/ppermute | solution.py:361
  30.7 15.9 %collective-permute-start.14 = (bf16[2,2,128,128]{3,2,1,0:T(8,128)(2,1)}, bf16[2,2,128,128]{3,2,1,0:T(8,128)(2,1)}, u32[]{:S(2)}, u32[]{:S(2)}) collective-permute-start(bf16[2,2,128,128]{3,2,1,0:T(8,128)(2,1)} %get-tuple-element.19), channel_id=1, source_target_pairs={{0,6},{1,7},{2,4},{3,5},{4,2},{5,3},{6,0},{7,1},{8,14},{9,15},{10,... | collective-permute-start | bytes 393224 | tf_op jit(solution)/shard_map/ppermute | solution.py:361
  33.5 20.7 %collective-permute-start.5 = (bf16[2,2,128,256]{3,2,1,0:T(8,128)(2,1)}, bf16[2,2,128,256]{3,2,1,0:T(8,128)(2,1)}, u32[]{:S(2)}, u32[]{:S(2)}) collective-permute-start(bf16[2,2,128,256]{3,2,1,0:T(8,128)(2,1)} %get-tuple-element.14), channel_id=1, source_target_pairs={{0,2},{1,3},{2,0},{3,1},{4,6},{5,7},{6,4},{7,5},{8,10},{9,11},{10,... | collective-permute-start | bytes 786440 | tf_op jit(solution)/shard_map/ppermute | solution.py:361
  38.9 15.2 %collective-permute-start.6 = (bf16[2,2,128,256]{3,2,1,0:T(8,128)(2,1)}, bf16[2,2,128,256]{3,2,1,0:T(8,128)(2,1)}, u32[]{:S(2)}, u32[]{:S(2)}) collective-permute-start(bf16[2,2,128,256]{3,2,1,0:T(8,128)(2,1)} %get-tuple-element.15), channel_id=1, source_target_pairs={{0,4},{1,5},{2,6},{3,7},{4,0},{5,1},{6,2},{7,3},{8,12},{9,13},{10,... | collective-permute-start | bytes 786440 | tf_op jit(solution)/shard_map/ppermute | solution.py:361
  38.9 15.2 %collective-permute-start.7 = (bf16[2,2,128,256]{3,2,1,0:T(8,128)(2,1)}, bf16[2,2,128,256]{3,2,1,0:T(8,128)(2,1)}, u32[]{:S(2)}, u32[]{:S(2)}) collective-permute-start(bf16[2,2,128,256]{3,2,1,0:T(8,128)(2,1)} %get-tuple-element.16), channel_id=1, source_target_pairs={{0,6},{1,7},{2,4},{3,5},{4,2},{5,3},{6,0},{7,1},{8,14},{9,15},{10,... | collective-permute-start | bytes 786440 | tf_op jit(solution)/shard_map/ppermute | solution.py:361
where the time goes:
time: 67.4 us; the launch traced here: 66.6 us
  Pallas kernels  30.6 us (45%)
  starting transfers between devices  17.1 us (25%)
  waiting for transfers between devices  14.9 us (22%)
  other arithmetic  2.43 us (4%)
  between operations  0.95 us (1%)
    pallas_call x3, Pallas kernels, attend(): pl.pallas_call(functools.partial(attend_kernel, first, heads, len(arrived...  27.3 us
    ppermute x18, starting transfers between devices, swap(): return lax.ppermute(x, 'seq', [(i, i ^ offset) for i in range(devices)])  17.1 us
    ppermute x18, waiting for transfers between devices, swap(): return lax.ppermute(x, 'seq', [(i, i ^ offset) for i in range(devices)])  14.9 us
    pallas_call x1, Pallas kernels, select_blocks(): pl.pallas_call(functools.partial(select_kernel, chips, rows), in_specs=[s...  3.28 us
  transfers between devices with their start and end apart: 18, of which 10 were waited for; matrix products, arithmetic and copies ran while one was open for 2% of the time, Pallas kernels for 27%

commit v1 on v0

--- a/solution.py
+++ b/solution.py
@@ -109,6 +109,20 @@
     fill = key_pool.shape[1] - 1
     width = GROUP * HEAD_SIZE
     me = me_ref[0]
+    cols = pl.ds(first * HEAD_SIZE, heads * HEAD_SIZE)
+    moves = [
+        (q_ref.at[:, pl.ds((first + h) * width, width)], q_buf.at[h]) for h in range(heads)
+    ]
+    moves += [
+        (own_k.at[:, cols], k_buf),
+        (own_v.at[:, cols], v_buf),
+        (reg_k.at[:, cols], reg_buf.at[0]),
+        (reg_v.at[:, cols], reg_buf.at[1]),
+    ]
+    moves += [(arrived[d], far_buf.at[d]) for d in range(received)]
+    copies = [pltpu.make_async_copy(x, y, sem.at[i]) for i, (x, y) in enumerate(moves)]
+    for copy in copies[heads:] + copies[:heads]:
+        copy.start()
     table = {}
     from_mate = jnp.int32(0)
     for b in range(blocks):
@@ -118,22 +132,12 @@
             table[b, t] = jnp.where(entry >= 0, blocks - 1 + away, fill)
             from_mate = jnp.where((entry >= 0) & (away == 1), entry % blocks, from_mate)
     start = pl.multiple_of(from_mate * rows, rows)
-    cols = pl.ds(first * HEAD_SIZE, heads * HEAD_SIZE)
-    moves = [
-        (q_ref.at[:, pl.ds((first + h) * width, width)], q_buf.at[h]) for h in range(heads)
-    ]
-    moves += [
-        (own_k.at[:, cols], k_buf),
-        (own_v.at[:, cols], v_buf),
-        (mate_k.at[pl.ds(start, rows), cols], mate_buf.at[0]),
-        (mate_v.at[pl.ds(start, rows), cols], mate_buf.at[1]),
-        (reg_k.at[:, cols], reg_buf.at[0]),
-        (reg_v.at[:, cols], reg_buf.at[1]),
-    ]
-    moves += [(arrived[d], far_buf.at[d]) for d in range(received)]
-    copies = [pltpu.make_async_copy(x, y, sem.at[i]) for i, (x, y) in enumerate(moves)]
-    for copy in copies:
+    for i, source in enumerate((mate_k, mate_v)):
+        copy = pltpu.make_async_copy(
+            source.at[pl.ds(start, rows), cols], mate_buf.at[i], sem.at[len(copies)]
+        )
         copy.start()
+        copies.append(copy)
     row_ids = lax.broadcasted_iota(jnp.int32, (ONES_ROWS, rows), 0)
     ones = jnp.where(row_ids == 0, 1.0, 0.0).astype(jnp.bfloat16)
     for h in range(heads):
@@ -252,15 +256,16 @@
             weights(i)
         if i >= 1:
             output(i - 1)
+    worst = over[0]
+    for other in over[1:]:
+        worst = jnp.maximum(worst, other)
+
+    unsafe = jnp.max(worst) * SCORE_SCALE > LARGEST_POWER
     for h in range(heads):
         for b in range(blocks):
             write(h, b).wait()
 
-    worst = over[0]
-    for other in over[1:]:
-        worst = jnp.maximum(worst, other)
-
-    @pl.when(jnp.max(worst) * SCORE_SCALE > LARGEST_POWER)
+    @pl.when(unsafe)
     def _():
         for h in range(heads):
 

time: 67.4 us -> 67 us (level)
  no operation moved by 1% of the time
where the time goes in v1:
time: 67 us; the launch traced here: 66.2 us
  Pallas kernels  30.2 us (45%)
  starting transfers between devices  17.1 us (26%)
  waiting for transfers between devices  14.9 us (22%)
  other arithmetic  2.43 us (4%)
  between operations  0.95 us (1%)
    pallas_call x3, Pallas kernels, attend(): pl.pallas_call(functools.partial(attend_kernel, first, heads, len(arrived...  26.9 us
    ppermute x18, starting transfers between devices, swap(): return lax.ppermute(x, 'seq', [(i, i ^ offset) for i in range(devices)])  17.1 us
    ppermute x18, waiting for transfers between devices, swap(): return lax.ppermute(x, 'seq', [(i, i ^ offset) for i in range(devices)])  14.9 us
    pallas_call x1, Pallas kernels, select_blocks(): pl.pallas_call(functools.partial(select_kernel, chips, rows), in_specs=[s...  3.28 us
  transfers between devices with their start and end apart: 18, of which 10 were waited for; matrix products, arithmetic and copies ran while one was open for 2% of the time, Pallas kernels for 27%

profile of v1, /device:TPU:0, one launch (start us, length us, event | category | flops | bytes accessed | tf_op | source)
XLA Modules:
  0.0 66.2 jit_solution(2204327078706815687)
XLA Ops:
  0.0 0.5 collective-permute-start
  0.5 0.0 collective-permute-start.1
  1.2 1.1 %collective-permute-done.refs_5_.refs_3_ = bf16[512,512]{1,0:T(8,128)(2,1)S(1)} collective-permute-done((bf16[512,512]{1,0:T(8,128)(2,1)}, bf16[512,512]{1,0:T(8,128)(2,1)S(1)}, u32[]{:S(2)}, u32[]{:S(2)}) %collective-permute-start) | collective-permute-done | bytes 524320 | tf_op jit(solution)/shard_map/ppermute | solution.py:366
  2.2 0.7 %collective-permute-done.1.refs_6_.refs_4_ = bf16[512,512]{1,0:T(8,128)(2,1)S(1)} collective-permute-done((bf16[512,512]{1,0:T(8,128)(2,1)}, bf16[512,512]{1,0:T(8,128)(2,1)S(1)}, u32[]{:S(2)}, u32[]{:S(2)}) %collective-permute-start.1) | collective-permute-done | bytes 524320 | tf_op jit(solution)/shard_map/ppermute | solution.py:366
  3.0 1.0 %fusion = bf16[64,512]{1,0:T(8,128)(2,1)S(1)} fusion(bf16[512,512]{1,0:T(8,128)(2,1)S(1)} %collective-permute-done.1.refs_6_.refs_4_, bf16[512,512]{1,0:T(8,128)(2,1)S(1)} %collective-permute-done.refs_5_.refs_3_, bf16[1,512,512]{2,1,0:T(8,128)(2,1)} %param.9, bf16[1,512,512]{2,1,0:T(8,128)(2,1)} %param.8, pred[]{:T(512)S(6)} %eq.20, pred[]{:T(512)S(6)} %eq.18), kind=kLoop, calls=%fused_computation.1 | loop fusion | flops 98304 | bytes 327682 | tf_op jit(solution)/shard_map/jit(_where)/select_n | solution.py:376
  4.0 2.9 %collective-permute-start.10 = (bf16[64,512]{1,0:T(8,128)(2,1)S(1)}, bf16[64,512]{1,0:T(8,128)(2,1)S(1)}, u32[]{:S(2)}, u32[]{:S(2)}) collective-permute-start(bf16[64,512]{1,0:T(8,128)(2,1)S(1)} %fusion), channel_id=1, source_target_pairs={{0,2},{1,3},{2,0},{3,1},{4,6},{5,7},{6,4},{7,5},{8,10},{9,11},{10,... | collective-permute-start | bytes 196616 | tf_op jit(solution)/shard_map/ppermute | solution.py:366
  6.9 1.5 %collective-permute-start.9 = (bf16[64,512]{1,0:T(8,128)(2,1)S(1)}, bf16[64,512]{1,0:T(8,128)(2,1)S(1)}, u32[]{:S(2)}, u32[]{:S(2)}) collective-permute-start(bf16[64,512]{1,0:T(8,128)(2,1)S(1)} %fusion), channel_id=1, source_target_pairs={{0,4},{1,5},{2,6},{3,7},{4,0},{5,1},{6,2},{7,3},{8,12},{9,13},{10,... | collective-permute-start | bytes 196616 | tf_op jit(solution)/shard_map/ppermute | solution.py:366
  8.4 0.0 collective-permute-start.8
  8.5 0.9 %collective-permute-done.10 = bf16[64,512]{1,0:T(8,128)(2,1)S(1)} collective-permute-done((bf16[64,512]{1,0:T(8,128)(2,1)S(1)}, bf16[64,512]{1,0:T(8,128)(2,1)S(1)}, u32[]{:S(2)}, u32[]{:S(2)}) %collective-permute-start.10) | collective-permute-done | bytes 65568 | tf_op jit(solution)/shard_map/ppermute | solution.py:366
  9.3 1.9 %collective-permute-done.9 = bf16[64,512]{1,0:T(8,128)(2,1)S(1)} collective-permute-done((bf16[64,512]{1,0:T(8,128)(2,1)S(1)}, bf16[64,512]{1,0:T(8,128)(2,1)S(1)}, u32[]{:S(2)}, u32[]{:S(2)}) %collective-permute-start.9) | collective-permute-done | bytes 65568 | tf_op jit(solution)/shard_map/ppermute | solution.py:366
  11.2 2.4 %collective-permute-done.8 = bf16[64,512]{1,0:T(8,128)(2,1)S(1)} collective-permute-done((bf16[64,512]{1,0:T(8,128)(2,1)S(1)}, bf16[64,512]{1,0:T(8,128)(2,1)S(1)}, u32[]{:S(2)}, u32[]{:S(2)}) %collective-permute-start.8) | collective-permute-done | bytes 65568 | tf_op jit(solution)/shard_map/ppermute | solution.py:366
  13.6 0.1 collective-permute-start.11
  13.7 0.8 %slice_select_fusion.2.listed = s32[4,7]{1,0:T(4,128)S(1)} fusion(s32[4,8]{1,0:T(4,128)} %bitcast.30, s32[4]{0:T(128)} %bitcast.31), kind=kLoop, calls=%fused_computation.6 | loop fusion | flops 56 | bytes 240 | tf_op jit(solution)/shard_map/jit(_where)/select_n | solution.py:369
  14.5 0.4 collective-permute-start.4
  14.9 1.6 %collective-permute-start.3 = (s32[4,7]{1,0:T(4,128)S(1)}, s32[4,7]{1,0:T(4,128)S(1)}, u32[]{:S(2)}, u32[]{:S(2)}) collective-permute-start(s32[4,7]{1,0:T(4,128)S(1)} %slice_select_fusion.2.listed), channel_id=1, source_target_pairs={{0,4},{1,5},{2,6},{3,7},{4,0},{5,1},{6,2},{7,3},{8,12},{9,13},{10,... | collective-permute-start | bytes 344 | tf_op jit(solution)/shard_map/ppermute | solution.py:366
  16.5 1.5 %collective-permute-start.2 = (s32[4,7]{1,0:T(4,128)S(1)}, s32[4,7]{1,0:T(4,128)S(1)}, u32[]{:S(2)}, u32[]{:S(2)}) collective-permute-start(s32[4,7]{1,0:T(4,128)S(1)} %slice_select_fusion.2.listed), channel_id=1, source_target_pairs={{0,2},{1,3},{2,0},{3,1},{4,6},{5,7},{6,4},{7,5},{8,10},{9,11},{10,... | collective-permute-start | bytes 344 | tf_op jit(solution)/shard_map/ppermute | solution.py:366
  17.9 1.0 %collective-permute-done.4.refs_2_ = s32[4,7]{1,0:T(4,128)S(1)} collective-permute-done((s32[4,7]{1,0:T(4,128)S(1)}, s32[4,7]{1,0:T(4,128)S(1)}, u32[]{:S(2)}, u32[]{:S(2)}) %collective-permute-start.4) | collective-permute-done | bytes 144 | tf_op jit(solution)/shard_map/ppermute | solution.py:366
  18.9 0.0 collective-permute-done.3.refs_1_
  18.9 1.1 %collective-permute-done.2.refs_0_ = s32[4,7]{1,0:T(4,128)S(1)} collective-permute-done((s32[4,7]{1,0:T(4,128)S(1)}, s32[4,7]{1,0:T(4,128)S(1)}, u32[]{:S(2)}, u32[]{:S(2)}) %collective-permute-start.2) | collective-permute-done | bytes 144 | tf_op jit(solution)/shard_map/ppermute | solution.py:366
  20.0 0.0 copy-done
  20.0 0.0 copy-done.1
  20.0 0.0 copy-done.3
  20.1 0.6 copy-done.5
  20.6 3.3 %select_blocks.1 = (bf16[2,2,128,128]{3,2,1,0:T(8,128)(2,1)}, bf16[2,2,128,128]{3,2,1,0:T(8,128)(2,1)}, bf16[2,2,128,128]{3,2,1,0:T(8,128)(2,1)}, bf16[2,2,128,1...) custom-call(s32[1]{0:T(128)} %bitcast.3.me_ref, ...), custom_call_target="tpu_custom_call" | custom-call | tf_op jit(solution)/shard_map/select_blocks/pallas_call | solution.py:79
  23.9 1.6 %collective-permute-start.12 = (bf16[2,2,128,128]{3,2,1,0:T(8,128)(2,1)}, bf16[2,2,128,128]{3,2,1,0:T(8,128)(2,1)}, u32[]{:S(2)}, u32[]{:S(2)}) collective-permute-start(bf16[2,2,128,128]{3,2,1,0:T(8,128)(2,1)} %get-tuple-element.17), channel_id=1, source_target_pairs={{0,2},{1,3},{2,0},{3,1},{4,6},{5,7},{6,4},{7,5},{8,10},{9,11},{10,... | collective-permute-start | bytes 393224 | tf_op jit(solution)/shard_map/ppermute | solution.py:366
  25.5 0.5 collective-permute-start.13
  26.0 0.5 collective-permute-start.15
  26.4 1.6 %collective-permute-start.16 = (bf16[2,2,128,128]{3,2,1,0:T(8,128)(2,1)}, bf16[2,2,128,128]{3,2,1,0:T(8,128)(2,1)}, u32[]{:S(2)}, u32[]{:S(2)}) collective-permute-start(bf16[2,2,128,128]{3,2,1,0:T(8,128)(2,1)} %get-tuple-element.21), channel_id=1, source_target_pairs={{0,4},{1,5},{2,6},{3,7},{4,0},{5,1},{6,2},{7,3},{8,12},{9,13},{10,... | collective-permute-start | bytes 393224 | tf_op jit(solution)/shard_map/ppermute | solution.py:366
  28.0 0.0 collective-permute-done.11
  28.0 1.4 %collective-permute-start.17 = (bf16[2,2,128,128]{3,2,1,0:T(8,128)(2,1)}, bf16[2,2,128,128]{3,2,1,0:T(8,128)(2,1)}, u32[]{:S(2)}, u32[]{:S(2)}) collective-permute-start(bf16[2,2,128,128]{3,2,1,0:T(8,128)(2,1)} %get-tuple-element.22), channel_id=1, source_target_pairs={{0,6},{1,7},{2,4},{3,5},{4,2},{5,3},{6,0},{7,1},{8,14},{9,15},{10,... | collective-permute-start | bytes 393224 | tf_op jit(solution)/shard_map/ppermute | solution.py:366
  29.5 0.7 broadcast_select_fusion
  30.1 0.0 copy-done.2
  30.1 0.5 collective-permute-done.12.refs_5_
  30.7 1.4 %collective-permute-start.14 = (bf16[2,2,128,128]{3,2,1,0:T(8,128)(2,1)}, bf16[2,2,128,128]{3,2,1,0:T(8,128)(2,1)}, u32[]{:S(2)}, u32[]{:S(2)}) collective-permute-start(bf16[2,2,128,128]{3,2,1,0:T(8,128)(2,1)} %get-tuple-element.19), channel_id=1, source_target_pairs={{0,6},{1,7},{2,4},{3,5},{4,2},{5,3},{6,0},{7,1},{8,14},{9,15},{10,... | collective-permute-start | bytes 393224 | tf_op jit(solution)/shard_map/ppermute | solution.py:366
  32.1 1.4 %collective-permute-done.15.refs_5_ = bf16[2,2,128,128]{3,2,1,0:T(8,128)(2,1)} collective-permute-done((bf16[2,2,128,128]{3,2,1,0:T(8,128)(2,1)}, bf16[2,2,128,128]{3,2,1,0:T(8,128)(2,1)}, u32[]{:S(2)}, u32[]{:S(2)}) %collective-permute-start.15) | collective-permute-done | bytes 131104 | tf_op jit(solution)/shard_map/ppermute | solution.py:366
  33.5 1.5 %collective-permute-start.5 = (bf16[2,2,128,256]{3,2,1,0:T(8,128)(2,1)}, bf16[2,2,128,256]{3,2,1,0:T(8,128)(2,1)}, u32[]{:S(2)}, u32[]{:S(2)}) collective-permute-start(bf16[2,2,128,256]{3,2,1,0:T(8,128)(2,1)} %get-tuple-element.14), channel_id=1, source_target_pairs={{0,2},{1,3},{2,0},{3,1},{4,6},{5,7},{6,4},{7,5},{8,10},{9,11},{10,... | collective-permute-start | bytes 786440 | tf_op jit(solution)/shard_map/ppermute | solution.py:366
  35.0 4.0 %collective-permute-done.16.refs_6_ = bf16[2,2,128,128]{3,2,1,0:T(8,128)(2,1)} collective-permute-done((bf16[2,2,128,128]{3,2,1,0:T(8,128)(2,1)}, bf16[2,2,128,128]{3,2,1,0:T(8,128)(2,1)}, u32[]{:S(2)}, u32[]{:S(2)}) %collective-permute-start.16) | collective-permute-done | bytes 131104 | tf_op jit(solution)/shard_map/ppermute | solution.py:366
  38.9 0.0 collective-permute-start.6
  38.9 0.0 collective-permute-done.17.refs_7_
  38.9 0.2 collective-permute-start.7
  39.1 7.4 %shard_map.73.refs_10_ = bf16[512,3584]{1,0:T(8,128)(2,1)} custom-call(s32[4,7]{1,0:T(4,128)} %copy-done.2, s32[4]{0:T(128)} %bitcast.27, s32[1]{0:T(128)} %bitcast.3.me_ref, bf16[512,3584]{1,0:T(8,128)(2,1)} %bitcast.14, bf16[512,512]{1,0:T(8,128)(2,1)} %bitcast.19, bf16[512,512]{1,0:T(8,128)(2,1)} %bitcast.24, bf16[512,512]{1,0:T(8,128)(2,1)} %copy-done, ...), custom_call_target="tpu_custom_call" | custom-call | flops 1996488704 | bytes 1835008 | tf_op jit(solution)/shard_map/pallas_call | solution.py:321
  46.5 0.0 collective-permute-done.13.refs_6_
  46.5 0.0 collective-permute-done.14.refs_7_
  46.5 7.4 %shard_map.74.refs_10_ = bf16[512,3584]{1,0:T(8,128)(2,1)} custom-call(s32[4,7]{1,0:T(4,128)} %copy-done.2, s32[4]{0:T(128)} %bitcast.28, s32[1]{0:T(128)} %bitcast.3.me_ref, bf16[512,3584]{1,0:T(8,128)(2,1)} %bitcast.15, bf16[512,512]{1,0:T(8,128)(2,1)} %bitcast.20, bf16[512,512]{1,0:T(8,128)(2,1)} %bitcast.25, ...), custom_call_target="tpu_custom_call", output_to_operand_aliasing={{}: (13, {})} | custom-call | flops 1996488704 | bytes 1835008 | tf_op jit(solution)/shard_map/pallas_call | solution.py:321
  54.0 0.0 collective-permute-done.5.refs_5_
  54.0 0.0 collective-permute-done.6.refs_6_
  54.0 0.0 collective-permute-done.7.refs_7_
  54.0 12.1 %shard_map.75 = bf16[512,3584]{1,0:T(8,128)(2,1)} custom-call(s32[4,7]{1,0:T(4,128)} %copy-done.2, s32[4]{0:T(128)} %bitcast.29, s32[1]{0:T(128)} %bitcast.3.me_ref, bf16[512,3584]{1,0:T(8,128)(2,1)} %bitcast.16, bf16[512,512]{1,0:T(8,128)(2,1)} %bitcast.21, bf16[512,512]{1,0:T(8,128)(2,1)} %bitcast.26, ...), custom_call_target="tpu_custom_call", output_to_operand_aliasing={{}: (13, {})} | custom-call | flops 3992977408 | bytes 3670016 | tf_op jit(solution)/shard_map/pallas_call | solution.py:321
  (8 shorter events, 0.0 us)
Async XLA Ops:
  0.0 2.2 %collective-permute-start = (bf16[512,512]{1,0:T(8,128)(2,1)}, bf16[512,512]{1,0:T(8,128)(2,1)S(1)}, u32[]{:S(2)}, u32[]{:S(2)}) collective-permute-start(bf16[512,512]{1,0:T(8,128)(2,1)} %bitcast.17), channel_id=1, source_target_pairs={{0,1},{1,0},{2,3},{3,2},{4,5},{5,4},{6,7},{7,6},{8,9},{9,8},{10,11... | collective-permute-start | bytes 1572872 | tf_op jit(solution)/shard_map/ppermute | solution.py:366
  0.5 2.5 %collective-permute-start.1 = (bf16[512,512]{1,0:T(8,128)(2,1)}, bf16[512,512]{1,0:T(8,128)(2,1)S(1)}, u32[]{:S(2)}, u32[]{:S(2)}) collective-permute-start(bf16[512,512]{1,0:T(8,128)(2,1)} %bitcast.22), channel_id=1, source_target_pairs={{0,1},{1,0},{2,3},{3,2},{4,5},{5,4},{6,7},{7,6},{8,9},{9,8},{10,11... | collective-permute-start | bytes 1572872 | tf_op jit(solution)/shard_map/ppermute | solution.py:366
  2.2 17.8 %copy-start = (bf16[512,512]{1,0:T(8,128)(2,1)}, bf16[512,512]{1,0:T(8,128)(2,1)S(1)}, u32[]{:S(2)}) copy-start(bf16[512,512]{1,0:T(8,128)(2,1)S(1)} %collective-permute-done.refs_5_.refs_3_) | copy-start | bytes 1572868
  3.0 17.1 %copy-start.1 = (bf16[512,512]{1,0:T(8,128)(2,1)}, bf16[512,512]{1,0:T(8,128)(2,1)S(1)}, u32[]{:S(2)}) copy-start(bf16[512,512]{1,0:T(8,128)(2,1)S(1)} %collective-permute-done.1.refs_6_.refs_4_) | copy-start | bytes 1572868
  4.0 5.3 %collective-permute-start.10 = (bf16[64,512]{1,0:T(8,128)(2,1)S(1)}, bf16[64,512]{1,0:T(8,128)(2,1)S(1)}, u32[]{:S(2)}, u32[]{:S(2)}) collective-permute-start(bf16[64,512]{1,0:T(8,128)(2,1)S(1)} %fusion), channel_id=1, source_target_pairs={{0,2},{1,3},{2,0},{3,1},{4,6},{5,7},{6,4},{7,5},{8,10},{9,11},{10,... | collective-permute-start | bytes 196616 | tf_op jit(solution)/shard_map/ppermute | solution.py:366
  6.9 4.3 %collective-permute-start.9 = (bf16[64,512]{1,0:T(8,128)(2,1)S(1)}, bf16[64,512]{1,0:T(8,128)(2,1)S(1)}, u32[]{:S(2)}, u32[]{:S(2)}) collective-permute-start(bf16[64,512]{1,0:T(8,128)(2,1)S(1)} %fusion), channel_id=1, source_target_pairs={{0,4},{1,5},{2,6},{3,7},{4,0},{5,1},{6,2},{7,3},{8,12},{9,13},{10,... | collective-permute-start | bytes 196616 | tf_op jit(solution)/shard_map/ppermute | solution.py:366
  8.4 5.2 %collective-permute-start.8 = (bf16[64,512]{1,0:T(8,128)(2,1)S(1)}, bf16[64,512]{1,0:T(8,128)(2,1)S(1)}, u32[]{:S(2)}, u32[]{:S(2)}) collective-permute-start(bf16[64,512]{1,0:T(8,128)(2,1)S(1)} %fusion), channel_id=1, source_target_pairs={{0,6},{1,7},{2,4},{3,5},{4,2},{5,3},{6,0},{7,1},{8,14},{9,15},{10,... | collective-permute-start | bytes 196616 | tf_op jit(solution)/shard_map/ppermute | solution.py:366
  13.6 14.4 %collective-permute-start.11 = (bf16[64,512]{1,0:T(8,128)(2,1)S(1)}, bf16[64,512]{1,0:T(8,128)(2,1)S(1)}, u32[]{:S(2)}, u32[]{:S(2)}) collective-permute-start(bf16[64,512]{1,0:T(8,128)(2,1)S(1)} %select_select_fusion), channel_id=1, source_target_pairs={{0,1},{1,0},{2,3},{3,2},{4,5},{5,4},{6,7},{7,6},{8,9},{9,8},{10,11... | collective-permute-start | bytes 196616 | tf_op jit(solution)/shard_map/ppermute | solution.py:366
  14.5 15.7 %copy-start.2 = (s32[4,7]{1,0:T(4,128)}, s32[4,7]{1,0:T(4,128)S(1)}, u32[]{:S(2)}) copy-start(s32[4,7]{1,0:T(4,128)S(1)} %slice_select_fusion.2.listed) | copy-start | bytes 340
  14.5 4.5 %collective-permute-start.4 = (s32[4,7]{1,0:T(4,128)S(1)}, s32[4,7]{1,0:T(4,128)S(1)}, u32[]{:S(2)}, u32[]{:S(2)}) collective-permute-start(s32[4,7]{1,0:T(4,128)S(1)} %slice_select_fusion.2.listed), channel_id=1, source_target_pairs={{0,6},{1,7},{2,4},{3,5},{4,2},{5,3},{6,0},{7,1},{8,14},{9,15},{10,... | collective-permute-start | bytes 344 | tf_op jit(solution)/shard_map/ppermute | solution.py:366
  14.9 4.1 %collective-permute-start.3 = (s32[4,7]{1,0:T(4,128)S(1)}, s32[4,7]{1,0:T(4,128)S(1)}, u32[]{:S(2)}, u32[]{:S(2)}) collective-permute-start(s32[4,7]{1,0:T(4,128)S(1)} %slice_select_fusion.2.listed), channel_id=1, source_target_pairs={{0,4},{1,5},{2,6},{3,7},{4,0},{5,1},{6,2},{7,3},{8,12},{9,13},{10,... | collective-permute-start | bytes 344 | tf_op jit(solution)/shard_map/ppermute | solution.py:366
  16.5 3.6 %collective-permute-start.2 = (s32[4,7]{1,0:T(4,128)S(1)}, s32[4,7]{1,0:T(4,128)S(1)}, u32[]{:S(2)}, u32[]{:S(2)}) collective-permute-start(s32[4,7]{1,0:T(4,128)S(1)} %slice_select_fusion.2.listed), channel_id=1, source_target_pairs={{0,2},{1,3},{2,0},{3,1},{4,6},{5,7},{6,4},{7,5},{8,10},{9,11},{10,... | collective-permute-start | bytes 344 | tf_op jit(solution)/shard_map/ppermute | solution.py:366
  18.9 1.1 %copy-start.3 = (s32[4,7]{1,0:T(4,128)}, s32[4,7]{1,0:T(4,128)S(1)}, u32[]{:S(2)}) copy-start(s32[4,7]{1,0:T(4,128)S(1)} %collective-permute-done.4.refs_2_) | copy-start | bytes 340
  18.9 1.1 %copy-start.4 = (s32[4,7]{1,0:T(4,128)}, s32[4,7]{1,0:T(4,128)S(1)}, u32[]{:S(2)}) copy-start(s32[4,7]{1,0:T(4,128)S(1)} %collective-permute-done.3.refs_1_) | copy-start | bytes 340
  20.0 0.6 copy-start.5
  23.9 6.8 %collective-permute-start.12 = (bf16[2,2,128,128]{3,2,1,0:T(8,128)(2,1)}, bf16[2,2,128,128]{3,2,1,0:T(8,128)(2,1)}, u32[]{:S(2)}, u32[]{:S(2)}) collective-permute-start(bf16[2,2,128,128]{3,2,1,0:T(8,128)(2,1)} %get-tuple-element.17), channel_id=1, source_target_pairs={{0,2},{1,3},{2,0},{3,1},{4,6},{5,7},{6,4},{7,5},{8,10},{9,11},{10,... | collective-permute-start | bytes 393224 | tf_op jit(solution)/shard_map/ppermute | solution.py:366
  25.5 21.1 %collective-permute-start.13 = (bf16[2,2,128,128]{3,2,1,0:T(8,128)(2,1)}, bf16[2,2,128,128]{3,2,1,0:T(8,128)(2,1)}, u32[]{:S(2)}, u32[]{:S(2)}) collective-permute-start(bf16[2,2,128,128]{3,2,1,0:T(8,128)(2,1)} %get-tuple-element.18), channel_id=1, source_target_pairs={{0,4},{1,5},{2,6},{3,7},{4,0},{5,1},{6,2},{7,3},{8,12},{9,13},{10,... | collective-permute-start | bytes 393224 | tf_op jit(solution)/shard_map/ppermute | solution.py:366
  26.0 7.5 %collective-permute-start.15 = (bf16[2,2,128,128]{3,2,1,0:T(8,128)(2,1)}, bf16[2,2,128,128]{3,2,1,0:T(8,128)(2,1)}, u32[]{:S(2)}, u32[]{:S(2)}) collective-permute-start(bf16[2,2,128,128]{3,2,1,0:T(8,128)(2,1)} %get-tuple-element.20), channel_id=1, source_target_pairs={{0,2},{1,3},{2,0},{3,1},{4,6},{5,7},{6,4},{7,5},{8,10},{9,11},{10,... | collective-permute-start | bytes 393224 | tf_op jit(solution)/shard_map/ppermute | solution.py:366
  26.4 12.5 %collective-permute-start.16 = (bf16[2,2,128,128]{3,2,1,0:T(8,128)(2,1)}, bf16[2,2,128,128]{3,2,1,0:T(8,128)(2,1)}, u32[]{:S(2)}, u32[]{:S(2)}) collective-permute-start(bf16[2,2,128,128]{3,2,1,0:T(8,128)(2,1)} %get-tuple-element.21), channel_id=1, source_target_pairs={{0,4},{1,5},{2,6},{3,7},{4,0},{5,1},{6,2},{7,3},{8,12},{9,13},{10,... | collective-permute-start | bytes 393224 | tf_op jit(solution)/shard_map/ppermute | solution.py:366
  28.0 10.9 %collective-permute-start.17 = (bf16[2,2,128,128]{3,2,1,0:T(8,128)(2,1)}, bf16[2,2,128,128]{3,2,1,0:T(8,128)(2,1)}, u32[]{:S(2)}, u32[]{:S(2)}) collective-permute-start(bf16[2,2,128,128]{3,2,1,0:T(8,128)(2,1)} %get-tuple-element.22), channel_id=1, source_target_pairs={{0,6},{1,7},{2,4},{3,5},{4,2},{5,3},{6,0},{7,1},{8,14},{9,15},{10,... | collective-permute-start | bytes 393224 | tf_op jit(solution)/shard_map/ppermute | solution.py:366
  30.7 15.9 %collective-permute-start.14 = (bf16[2,2,128,128]{3,2,1,0:T(8,128)(2,1)}, bf16[2,2,128,128]{3,2,1,0:T(8,128)(2,1)}, u32[]{:S(2)}, u32[]{:S(2)}) collective-permute-start(bf16[2,2,128,128]{3,2,1,0:T(8,128)(2,1)} %get-tuple-element.19), channel_id=1, source_target_pairs={{0,6},{1,7},{2,4},{3,5},{4,2},{5,3},{6,0},{7,1},{8,14},{9,15},{10,... | collective-permute-start | bytes 393224 | tf_op jit(solution)/shard_map/ppermute | solution.py:366
  33.5 20.5 %collective-permute-start.5 = (bf16[2,2,128,256]{3,2,1,0:T(8,128)(2,1)}, bf16[2,2,128,256]{3,2,1,0:T(8,128)(2,1)}, u32[]{:S(2)}, u32[]{:S(2)}) collective-permute-start(bf16[2,2,128,256]{3,2,1,0:T(8,128)(2,1)} %get-tuple-element.14), channel_id=1, source_target_pairs={{0,2},{1,3},{2,0},{3,1},{4,6},{5,7},{6,4},{7,5},{8,10},{9,11},{10,... | collective-permute-start | bytes 786440 | tf_op jit(solution)/shard_map/ppermute | solution.py:366
  38.9 15.1 %collective-permute-start.6 = (bf16[2,2,128,256]{3,2,1,0:T(8,128)(2,1)}, bf16[2,2,128,256]{3,2,1,0:T(8,128)(2,1)}, u32[]{:S(2)}, u32[]{:S(2)}) collective-permute-start(bf16[2,2,128,256]{3,2,1,0:T(8,128)(2,1)} %get-tuple-element.15), channel_id=1, source_target_pairs={{0,4},{1,5},{2,6},{3,7},{4,0},{5,1},{6,2},{7,3},{8,12},{9,13},{10,... | collective-permute-start | bytes 786440 | tf_op jit(solution)/shard_map/ppermute | solution.py:366
  38.9 15.1 %collective-permute-start.7 = (bf16[2,2,128,256]{3,2,1,0:T(8,128)(2,1)}, bf16[2,2,128,256]{3,2,1,0:T(8,128)(2,1)}, u32[]{:S(2)}, u32[]{:S(2)}) collective-permute-start(bf16[2,2,128,256]{3,2,1,0:T(8,128)(2,1)} %get-tuple-element.16), channel_id=1, source_target_pairs={{0,6},{1,7},{2,4},{3,5},{4,2},{5,3},{6,0},{7,1},{8,14},{9,15},{10,... | collective-permute-start | bytes 786440 | tf_op jit(solution)/shard_map/ppermute | solution.py:366
